TPU v7x, 32 devices: a 4x2x2 block of a 4x4x8 slice. The times are simulated.
32 devices in a mesh: dp: 4 (over y, z), tp: 8 (over x, core).
Axes of the slice: x: 4, y: 2, z: 2, core: 2. Of those that a mesh axis runs over, the one named last changes fastest.
The devices are a block of a 4x4x8 slice.
Arguments:
- hidden: bfloat16 [16384, 768], P(('dp', 'tp')), parts along dimension 0
- ln_gamma: float32 [768], replicated
- ln_beta: float32 [768], replicated
- out_embed: bfloat16 [51200, 768], P('tp')
- vocab_valid: int32 [51200], P('tp')
- targets: int32 [16384], P(('dp', 'tp')), parts along dimension 0
- loss_mask: int32 [16384], P(('dp', 'tp')), parts along dimension 0
Outputs:
- output 1: float32 [16384], P(('dp', 'tp')), parts along dimension 0
- output 2: float32 [4], P('dp'), parts along dimension 0
- output 3: bfloat16 [16384, 768], P(('dp', 'tp')), parts along dimension 0
- output 4: float32 [204800, 768], P(('dp', 'tp')), parts along dimension 0
- output 5: float32 [3072], P('dp'), parts along dimension 0
- output 6: float32 [3072], P('dp'), parts along dimension 0
There are 4 independent parts. A program takes and returns all parts, laid end to end along the dimension named above; an argument that names none is the same for every part.
All inputs are finite; a program needn't handle non-finite values.
Results may differ from a plain program's by a relative error of at most 0.001.
Values are sent between devices in bfloat16 or wider.
A program may use at most 768 MiB of HBM per device.

v0:
```python
import jax
import jax.numpy as jnp
from jax import lax
from jax.sharding import PartitionSpec as P

LN_EPS = 1e-5


def layer_norm(hidden32, ln_gamma, ln_beta):
    row_mean = jnp.mean(hidden32, axis=-1, keepdims=True)
    centered = hidden32 - row_mean
    row_var = jnp.mean(centered * centered, axis=-1, keepdims=True)
    return centered * lax.rsqrt(row_var + LN_EPS) * ln_gamma + ln_beta


def solution(mesh):
    tok_spec = P(("dp", "tp"))
    row_spec = P(("dp", "tp"), None)

    def local_step(hidden_blk, ln_gamma, ln_beta, embed_blk, valid_blk, tgt_blk, mask_blk):
        tok_local = hidden_blk.shape[0]
        shard_vocab = embed_blk.shape[0]
        shard_idx = lax.axis_index("tp")
        normed, ln_vjp = jax.vjp(layer_norm, hidden_blk.astype(jnp.float32), ln_gamma, ln_beta)
        x_all = lax.all_gather(normed.astype(jnp.bfloat16), "tp", axis=0, tiled=True)
        labels = lax.all_gather(jnp.stack([tgt_blk, mask_blk]), "tp", axis=1, tiled=True)
        weight = labels[1].astype(jnp.float32)
        logits = lax.dot_general(x_all, embed_blk, (((1,), (1,)), ((), ())), preferred_element_type=jnp.float32)
        allowed = (valid_blk > 0)[None, :]
        local_max = jnp.max(jnp.where(allowed, logits, -jnp.inf), axis=1)
        row_max = lax.pmax(local_max, "tp")
        shifted_exp = jnp.where(allowed, jnp.exp(logits - row_max[:, None]), 0.0)
        target_hit = (jnp.arange(shard_vocab) + shard_idx * shard_vocab)[None, :] == labels[0][:, None]
        picked_part = jnp.sum(jnp.where(target_hit, logits, 0.0), axis=1)
        tok_stats = lax.psum(jnp.stack([jnp.sum(shifted_exp, axis=1), picked_part]), "tp")
        log_norm = row_max + jnp.log(tok_stats[0])
        tok_count = jnp.sum(weight)
        tok_loss = (log_norm - tok_stats[1]) * weight
        mean_loss = (jnp.sum(tok_loss) / tok_count).reshape(1)
        soft_probs = shifted_exp / tok_stats[0][:, None]
        d_logits = ((soft_probs - target_hit.astype(jnp.float32)) * (weight / tok_count)[:, None]).astype(jnp.bfloat16)
        d_embed = lax.dot_general(d_logits, x_all, (((0,), (0,)), ((), ())), preferred_element_type=jnp.float32)
        dx_part = jnp.dot(d_logits, embed_blk, preferred_element_type=jnp.float32)
        dx_local = lax.psum_scatter(dx_part, "tp", scatter_dimension=0, tiled=True)
        d_hidden, d_gamma, d_beta = ln_vjp(dx_local)
        ln_grads = lax.psum(jnp.stack([d_gamma, d_beta]), "tp")
        loss_local = lax.dynamic_slice_in_dim(tok_loss, shard_idx * tok_local, tok_local)
        return loss_local, mean_loss, d_hidden.astype(jnp.bfloat16), d_embed, ln_grads[0], ln_grads[1]

    return jax.shard_map(local_step, mesh=mesh, in_specs=(row_spec, P(), P(), P("tp", None), P("tp"), tok_spec, tok_spec), out_specs=(tok_spec, P("dp"), row_spec, row_spec, P("dp"), P("dp")), check_vma=False)
```

profile of v0, /device:TPU:81, one launch (start us, length us, event | category | flops | bytes accessed | tf_op | source)
XLA Modules:
  0.0 393.7 jit_solution(871739971656341545)
XLA Ops:
  7.2 0.1 all-gather.2.cloned.1.call-start
  7.2 1.3 convert_reduce_fusion
  8.6 0.0 copy-start.1
  8.6 1.5 fusion.14
  10.1 0.0 copy-start.6
  10.1 0.6 copy-done.6
  10.7 0.6 copy-done.4
  11.3 2.4 fusion.12
  13.6 0.1 all-gather.2.cloned.1.call-update
  13.7 0.1 reduce-scatter.2.cloned.1.call-start
  13.8 0.7 pad_add_fusion
  14.5 14.8 %all_gather.7 = s32[2,4096]{1,0:T(2,128)S(1)} all-gather(s32[2,512]{1,0:T(2,128)S(1)} %pad_add_fusion), channel_id=1, replica_groups=mesh['dp'=4,'tp'=8] {'tp'}, dimensions={1}, use_global_device_ids=true | all-gather | bytes 36864 | tf_op jit(solution)/shard_map/all_gather | solution.py:26
  29.3 0.6 fusion.17
  29.9 0.8 broadcast_compare_fusion
  30.7 25.2 %all-gather.2.cloned.1.call-done = bf16[4096,768]{1,0:T(8,128)(2,1)} async-done(((bf16[512,768]{1,0:T(8,128)(2,1)}), bf16[4096,768]{1,0:T(8,128)(2,1)}) %all-gather.2.cloned.1.call-update) | async-done | bytes 6291472 | tf_op jit(solution)/shard_map/all_gather | solution.py:25
  55.9 52.9 %select_reduce_fusion = (f32[4096]{0:T(1024)S(1)}, f32[4096,6400]{1,0:T(8,128)}) fusion(pred[6400]{0:T(1024)(128)(4,1)S(1)} %broadcast_compare_fusion, bf16[4096,768]{1,0:T(8,128)(2,1)} %all-gather.2.cloned.1.call-done, bf16[6400,768]{1,0:T(8,128)(2,1)} %param.10), kind=kOutput, calls=%fused_computation.7 | convolution fusion | flops 40317743104 | bytes 121002240 | tf_op jit(solution)/shard_map/dot_general | solution.py:28
  108.8 20.8 %pmax.7 = f32[4096]{0:T(1024)S(1)} all-reduce(f32[4096]{0:T(1024)S(1)} %get-tuple-element.22), channel_id=1, replica_groups=mesh['dp'=4,'tp'=8] {'tp'}, use_global_device_ids=true, to_apply=%region_3.4 | all-reduce | flops 4096 | bytes 32768 | tf_op jit(solution)/shard_map/pmax | solution.py:31
  129.7 39.4 %fusion.4 = (f32[4096]{0:T(1024)S(1)}, f32[4096]{0:T(1024)S(1)}) fusion(f32[4096,6400]{1,0:T(8,128)} %get-tuple-element.23, f32[4096]{0:T(1024)S(1)} %pmax.7, pred[6400]{0:T(1024)(128)(4,1)S(1)} %broadcast_compare_fusion, s32[4096]{0:T(1024)S(1)} %bitcast.15, s32[6400]{0:T(1024)S(1)} %iota_add_fusion), kind=kLoop, calls=%fused_computation.8 | loop fusion | flops 157278208 | bytes 104955136 | tf_op jit(solution)/shard_map/reduce_sum | solution.py:35
  169.1 23.7 %psum.14 = f32[2,4096]{1,0:T(2,128)S(1)} all-reduce(f32[2,4096]{1,0:T(2,128)S(1)} %pad_maximum_fusion), channel_id=1, replica_groups=mesh['dp'=4,'tp'=8] {'tp'}, use_global_device_ids=true, to_apply=%region_6.7 | all-reduce | flops 8192 | bytes 65536 | tf_op jit(solution)/shard_map/psum | solution.py:35
  192.8 1.3 fusion.19
  194.0 51.6 %fusion.3 = bf16[4096,6400]{1,0:T(8,128)(2,1)} fusion(f32[4096,6400]{1,0:T(8,128)} %get-tuple-element.23, f32[4096]{0:T(1024)S(1)} %get-tuple-element.21, f32[4096]{0:T(1024)S(1)} %bitcast.18, s32[6400]{0:T(1024)S(1)} %iota_add_fusion, f32[4096]{0:T(1024)S(1)} %pmax.7, s32[4096]{0:T(1024)S(1)} %bitcast.16, pred[6400]{0:T(1024)(128)(4,1)S(1)} %broadcast_compare_fusion), kind=kLoop, calls=%fused_computation.5 | loop fusion | flops 209715200 | bytes 157383936 | tf_op jit(solution)/shard_map/convert_element_type | solution.py:41
  245.6 50.1 %fusion.22 = f32[4096,768]{1,0:T(8,128)} fusion(bf16[4096,6400]{1,0:T(8,128)(2,1)} %fusion.3, bf16[6400,768]{1,0:T(8,128)(2,1)} %param.10), kind=kOutput, calls=%fused_computation.44 | convolution fusion | flops 40265318400 | bytes 74842112 | tf_op jit(solution)/shard_map/dot_general | solution.py:43
  295.7 0.1 reduce-scatter.2.cloned.1.call-update
  297.1 0.7 dynamic_slice.3
  297.8 51.5 %fusion.23 = f32[6400,768]{1,0:T(8,128)} fusion(bf16[4096,6400]{1,0:T(8,128)(2,1)} %fusion.3, bf16[4096,768]{1,0:T(8,128)(2,1)} %all-gather.2.cloned.1.call-done), kind=kOutput, calls=%fused_computation.45 | convolution fusion | flops 40265318400 | bytes 78381056 | tf_op jit(solution)/shard_map/dot_general | solution.py:42
  349.3 17.4 %reduce-scatter.2.cloned.1.call-done = f32[512,768]{1,0:T(8,128)} async-done(((f32[4096,768]{1,0:T(8,128)}), f32[512,768]{1,0:T(8,128)}) %reduce-scatter.2.cloned.1.call-update) | async-done | bytes 1572880 | tf_op jit(solution)/shard_map/reduce_scatter | solution.py:44
  366.7 0.0 copy-done.2
  366.7 2.1 fusion.13
  368.8 2.1 fusion.18
  370.9 13.1 %psum.15 = f32[2,768]{1,0:T(2,128)S(1)} all-reduce(f32[2,768]{1,0:T(2,128)S(1)} %pad_maximum_fusion.1), channel_id=1, replica_groups=mesh['dp'=4,'tp'=8] {'tp'}, use_global_device_ids=true, to_apply=%region_14.15 | all-reduce | flops 1536 | bytes 12288 | tf_op jit(solution)/shard_map/psum | solution.py:46
  384.1 0.6 slice_reduce_fusion
  384.7 1.0 add_convert_fusion
  (22 shorter events, 0.2 us)
Async XLA Ops:
  7.2 48.7 %all-gather.2.cloned.1.call-start = ((), (), s32[]{:S(2)}) async-start(), calls=%async_computation.1 | async-start | bytes 7077888 | tf_op jit(solution)/shard_map/all_gather | solution.py:25
  8.6 2.1 copy-start.1
  10.1 0.6 copy-start.6
  10.7 0.6 copy-start.4
  13.7 353.0 %reduce-scatter.2.cloned.1.call-start = ((), (), s32[]{:S(2)}) async-start(), calls=%async_computation.2 | async-start | bytes 14155776 | tf_op jit(solution)/shard_map/reduce_scatter | solution.py:44
  297.8 68.9 %copy-start = (bf16[512,768]{1,0:T(8,128)(2,1)S(1)}, bf16[512,768]{1,0:T(8,128)(2,1)}, u32[]{:S(2)}) copy-start(bf16[512,768]{1,0:T(8,128)(2,1)} %param.7) | copy-start | bytes 2359300
  297.8 68.9 %copy-start.2 = (f32[512]{0:T(512)S(1)}, f32[512]{0:T(512)}, u32[]{:S(2)}) copy-start(f32[512]{0:T(512)} %copy-done.1) | copy-start | bytes 6148
  297.8 68.9 %copy-start.3 = (f32[768]{0:T(1024)S(1)}, f32[768]{0:T(1024)}, u32[]{:S(2)}) copy-start(f32[768]{0:T(1024)} %param.8) | copy-start | bytes 9220
  297.8 68.9 %copy-start.5 = (f32[512]{0:T(512)S(1)}, f32[512]{0:T(512)}, u32[]{:S(2)}) copy-start(f32[512]{0:T(512)} %copy-done.4) | copy-start | bytes 6148
  297.8 71.0 %copy-start.7 = (f32[512]{0:T(512)S(1)}, f32[512]{0:T(512)}, u32[]{:S(2)}) copy-start(f32[512]{0:T(512)} %copy-done.6) | copy-start | bytes 6148
Sparse Core Ops, SparseCore 0:
  13.8 42.0 all-gather.1
  295.9 70.7 reduce-scatter.1
where the time goes:
time: 394 us
  matrix products  155 us (39%)
  other arithmetic  105 us (27%)
  blocking collectives  72.4 us (18%)
  waiting for transfers between devices  42.7 us (11%)
  between operations  16.7 us (4%)
    dot_general x1, matrix products, local_step(): lax.dot_general(x_all, embed_blk, (((1,), (1,)), ((), ())), preferred_ele...  52.9 us
    convert_element_type x1, other arithmetic, local_step(): ((soft_probs - target_hit.astype(jnp.float32)) * (weight / tok_count)[:,...  51.6 us
    dot_general x1, matrix products, local_step(): lax.dot_general(d_logits, x_all, (((0,), (0,)), ((), ())), preferred_elem...  51.5 us
    dot_general x1, matrix products, local_step(): dx_part = jnp.dot(d_logits, embed_blk, preferred_element_type=jnp.float32)  50.1 us
    reduce_sum x1, other arithmetic, local_step(): jnp.sum(shifted_exp, axis=1)  39.4 us
    all_gather x1, waiting for transfers between devices, local_step(): lax.all_gather(normed.astype(jnp.bfloat16), 'tp', axis=0, tiled=True)  25.2 us
    psum x1, blocking collectives, local_step(): lax.psum(jnp.stack([jnp.sum(shifted_exp, axis=1), picked_part]), 'tp')  23.7 us
    pmax x1, blocking collectives, local_step(): row_max = lax.pmax(local_max, 'tp')  20.8 us
  transfers between devices with their start and end apart: 2, of which 2 were waited for; matrix products, arithmetic and copies ran while one was open for 14% of the time, Pallas kernels for 0%

commit v1 on v0

v1 whole, which is shorter than its diff:
```python
import functools

import jax
import jax.numpy as jnp
from jax import lax
from jax.experimental import pallas as pl
from jax.experimental.pallas import tpu as pltpu
from jax.sharding import PartitionSpec as P

LN_EPS = 1e-5
LOG2E = 1.4426950408889634
LN2 = 0.6931471805599453
LOW = -3.0e38
TV = 1280
TT = 512
ANY = pl.BlockSpec(memory_space=pl.ANY)
VM = pl.BlockSpec(memory_space=pltpu.VMEM)
VMEM_LIMIT = 64000 * 1024


def layer_norm(hidden32, ln_gamma, ln_beta):
    row_mean = jnp.mean(hidden32, axis=-1, keepdims=True)
    centered = hidden32 - row_mean
    row_var = jnp.mean(centered * centered, axis=-1, keepdims=True)
    return centered * lax.rsqrt(row_var + LN_EPS) * ln_gamma + ln_beta


def cols(start, size=TT):
    return pl.ds(pl.multiple_of(start, 128), size)


def tile_stats(z_ref, base, col, tgt_ref, m_ref, s_ref, p_ref):
    rows, tokens = z_ref.shape
    at = cols(col, tokens)
    rel = jnp.broadcast_to(tgt_ref[:, at], (8, tokens)) - lax.broadcasted_iota(jnp.int32, (8, tokens), 0) - base
    m_old = m_ref[:, at]
    m_new = m_old
    for r in range(0, rows, 8):
        m_new = jnp.maximum(m_new, z_ref[r:r + 8])
    s = s_ref[:, at] * jnp.exp2(m_old - m_new)
    picked = p_ref[:, at]
    for r in range(0, rows, 8):
        z = z_ref[r:r + 8]
        s = s + jnp.exp2(z - m_new)
        picked = picked + jnp.where(rel == r, z, 0.0)
    m_ref[:, at] = m_new
    s_ref[:, at] = s
    p_ref[:, at] = picked


def forward_kernel(e_ref, bias_ref, x_ref, tgt_ref, z_hbm, m_ref, s_ref, p_ref, *rest):
    nv, nt = e_ref.shape[0] // TV, x_ref.shape[0] // TT
    zb, out_sem = rest[:nv], rest[nv]
    m_ref[...] = jnp.full(m_ref.shape, LOW, jnp.float32)
    s_ref[...] = jnp.zeros(s_ref.shape, jnp.float32)
    p_ref[...] = jnp.zeros(p_ref.shape, jnp.float32)
    zb[-1][...] = jnp.full(zb[-1].shape, -jnp.inf, jnp.float32)

    def out(k, t):
        return pltpu.make_async_copy(zb[k], z_hbm.at[t * nv + k], out_sem.at[k])

    for k in range(nv):
        out(k, 0).start()

    def body(t, carry):
        x_blk = x_ref[pl.ds(pl.multiple_of(t * TT, TT), TT), :]
        for v in range(nv):
            out(v, 0).wait()
            at = slice(v * TV, (v + 1) * TV)
            z = lax.dot_general(e_ref[at, :], x_blk, (((1,), (1,)), ((), ())), preferred_element_type=jnp.float32)
            zb[v][...] = z * LOG2E + jnp.concatenate([bias_ref[at, :]] * (TT // 128), axis=1)
            prev = (v - 1) % nv
            t_prev = t if v else jnp.maximum(t - 1, 0)
            base = prev * TV if v else jnp.where(t > 0, prev * TV, -(1 << 30))
            tile_stats(zb[prev], base, t_prev * TT, tgt_ref, m_ref, s_ref, p_ref)
            out(v, t).start()
        return carry

    lax.fori_loop(0, nt, body, 0)
    tile_stats(zb[-1], (nv - 1) * TV, (nt - 1) * TT, tgt_ref, m_ref, s_ref, p_ref)
    for k in range(nv):
        out(k, 0).wait()


def forward(embed, bias, x_all, tgt):
    v, t, d = embed.shape[0], x_all.shape[0], x_all.shape[1]
    nv = v // TV
    stat = jax.ShapeDtypeStruct((8, t), jnp.float32)
    return pl.pallas_call(
        forward_kernel,
        out_shape=(jax.ShapeDtypeStruct((nv * (t // TT), TV, TT), jnp.float32), stat, stat, stat),
        in_specs=[VM] * 4,
        out_specs=(ANY, VM, VM, VM),
        scratch_shapes=[pltpu.VMEM((TV, TT), jnp.float32)] * nv + [pltpu.SemaphoreType.DMA((nv,))],
        compiler_params=pltpu.CompilerParams(vmem_limit_bytes=VMEM_LIMIT),
        cost_estimate=pl.CostEstimate(flops=2 * v * t * d, bytes_accessed=4 * v * t, transcendentals=v * t),
        name="logits",
    )(embed, bias, x_all, tgt)


def tile_grad(z_ref, dz_ref, base, col, lse_ref, w_ref, tgt_ref):
    rows, tokens = z_ref.shape
    for c in range(0, tokens, 128):
        at = cols(col + c, 128)
        lse = jnp.broadcast_to(lse_ref[:, at], (8, 128))
        w = jnp.broadcast_to(w_ref[:, at], (8, 128))
        rel = jnp.broadcast_to(tgt_ref[:, at], (8, 128)) - lax.broadcasted_iota(jnp.int32, (8, 128), 0) - base
        for r in range(0, rows, 16):
            pair = []
            for q in (r, r + 8):
                p = jnp.exp2(z_ref[q:q + 8, c:c + 128] - lse)
                pair.append(p - jnp.where(rel == q, w, 0.0))
            dz_ref[r:r + 16, c:c + 128] = jnp.concatenate(pair, axis=0).astype(jnp.bfloat16)


def dx_kernel(et_ref, lse_ref, w_ref, tgt_ref, z_hbm, dx_hbm, *rest):
    nv, nt = et_ref.shape[1] // TV, lse_ref.shape[1] // TT
    n = nv * nt
    zb, db = rest[:nv], rest[nv:nv + 2]
    acc, z_sem, x_sem = rest[nv + 2:]

    def z_in(k, g):
        return pltpu.make_async_copy(z_hbm.at[g], zb[k], z_sem.at[k])

    def x_out(par, t):
        return pltpu.make_async_copy(acc.at[par], dx_hbm.at[t], x_sem.at[par])

    def grad(v, t, d_ref):
        tile_grad(zb[v], d_ref, v * TV, t * TT, lse_ref, w_ref, tgt_ref)

    for k in range(nv):
        z_in(k, k).start()
    for k in range(2):
        x_out(k, k).start()
    z_in(0, 0).wait()
    grad(0, 0, db[0])
    z_in(0, nv).start()

    def block(t, par):
        x_out(par, 0).wait()
        for v in range(nv):
            cur, nxt = db[(par * nv + v) % 2], db[(par * nv + v + 1) % 2]
            vn = (v + 1) % nv
            tn = t if v + 1 < nv else jnp.minimum(t + 1, nt - 1)
            z_in(vn, 0).wait()
            d = jnp.dot(et_ref[:, v * TV:(v + 1) * TV], cur[...], preferred_element_type=jnp.float32)
            acc[par] = d if v == 0 else acc[par] + d
            grad(vn, tn, nxt)
            z_in(vn, jnp.minimum((tn + 1) * nv + vn, n - nv + vn)).start()
        x_out(par, t).start()

    def body(i, carry):
        block(2 * i, 0)
        block(2 * i + 1, 1)
        return carry

    lax.fori_loop(0, nt // 2, body, 0)
    for k in range(nv):
        z_in(k, 0).wait()
    for k in range(2):
        x_out(k, 0).wait()


def token_grad(embed_t, lse, w, tgt, z):
    (d, v), t = embed_t.shape, lse.shape[1]
    nv = v // TV
    return pl.pallas_call(
        dx_kernel,
        out_shape=jax.ShapeDtypeStruct((t // TT, d, TT), jnp.float32),
        in_specs=[VM] * 4 + [ANY],
        out_specs=ANY,
        scratch_shapes=[pltpu.VMEM((TV, TT), jnp.float32)] * nv
        + [pltpu.VMEM((TV, TT), jnp.bfloat16)] * 2
        + [pltpu.VMEM((2, d, TT), jnp.float32), pltpu.SemaphoreType.DMA((nv,)), pltpu.SemaphoreType.DMA((2,))],
        compiler_params=pltpu.CompilerParams(vmem_limit_bytes=VMEM_LIMIT),
        cost_estimate=pl.CostEstimate(flops=2 * v * t * d, bytes_accessed=4 * v * t, transcendentals=v * t),
        name="token_grad",
    )(embed_t, lse, w, tgt, z)


def de_kernel(z_ref, x_ref, lse_ref, w_ref, tgt_ref, o_ref):
    v, t = pl.program_id(0), pl.program_id(1)
    at = cols(t * TT)
    lse = lse_ref[:, at]
    w = jnp.broadcast_to(w_ref[:, at], (8, TT))
    rel = jnp.broadcast_to(tgt_ref[:, at], (8, TT)) - lax.broadcasted_iota(jnp.int32, (8, TT), 0) - v * TV
    x_blk = x_ref[pl.ds(pl.multiple_of(t * TT, TT), TT), :]

    @pl.when(t == 0)
    def _():
        o_ref[...] = jnp.zeros_like(o_ref)

    for k in range(0, TV, 256):
        p = jnp.exp2(z_ref[0, k:k + 256] - lse)
        dz = jnp.concatenate([p[r:r + 8] - jnp.where(rel == k + r, w, 0.0) for r in range(0, 256, 8)], axis=0)
        o_ref[k:k + 256] += jnp.dot(dz.astype(jnp.bfloat16), x_blk, preferred_element_type=jnp.float32)


def embed_grad(z, x_all, lse, w, tgt, v):
    t, d = x_all.shape
    nv = v // TV
    return pl.pallas_call(
        de_kernel,
        grid=(nv, t // TT),
        out_shape=jax.ShapeDtypeStruct((v, d), jnp.float32),
        in_specs=[pl.BlockSpec((1, TV, TT), lambda i, j: (j * nv + i, 0, 0))] + [VM] * 4,
        out_specs=pl.BlockSpec((TV, d), lambda i, j: (i, 0)),
        compiler_params=pltpu.CompilerParams(vmem_limit_bytes=VMEM_LIMIT),
        cost_estimate=pl.CostEstimate(flops=2 * v * t * d, bytes_accessed=4 * v * t + 4 * v * d, transcendentals=v * t),
        name="embed_grad",
    )(z, x_all, lse, w, tgt)


def norm_grad_kernel(h_ref, gamma_ref, dxt_ref, dh_ref, g_ref):
    h = h_ref[...].astype(jnp.float32)
    mean = jnp.mean(h, axis=1, keepdims=True)
    cen = h - mean
    rstd = lax.rsqrt(jnp.mean(cen * cen, axis=1, keepdims=True) + LN_EPS)
    xhat = cen * rstd
    dy = dxt_ref[...].T
    g_ref[0:1, :] = jnp.sum(dy * xhat, axis=0, keepdims=True)
    g_ref[1:2, :] = jnp.sum(dy, axis=0, keepdims=True)
    dn = dy * gamma_ref[...]
    dh = rstd * (dn - jnp.mean(dn, axis=1, keepdims=True) - xhat * jnp.mean(dn * xhat, axis=1, keepdims=True))
    dh_ref[...] = dh.astype(jnp.bfloat16)


def norm_grad(hidden, gamma, dx_t):
    t, d = hidden.shape
    return pl.pallas_call(
        norm_grad_kernel,
        out_shape=(jax.ShapeDtypeStruct((t, d), jnp.bfloat16), jax.ShapeDtypeStruct((2, d), jnp.float32)),
        in_specs=[VM] * 3,
        out_specs=(VM, VM),
        compiler_params=pltpu.CompilerParams(vmem_limit_bytes=VMEM_LIMIT),
        name="norm_grad",
    )(hidden, gamma[None, :], dx_t)


def solution(mesh):
    tok_spec = P(("dp", "tp"))
    row_spec = P(("dp", "tp"), None)

    def local_step(hidden_blk, ln_gamma, ln_beta, embed_blk, valid_blk, tgt_blk, mask_blk):
        tok_local = hidden_blk.shape[0]
        shard_vocab = embed_blk.shape[0]
        shard_idx = lax.axis_index("tp")
        normed = layer_norm(hidden_blk.astype(jnp.float32), ln_gamma, ln_beta)
        x_all = lax.all_gather(normed.astype(jnp.bfloat16), "tp", axis=0, tiled=True)
        labels = lax.all_gather(jnp.stack([tgt_blk, mask_blk]), "tp", axis=1, tiled=True)
        weight = labels[1].astype(jnp.float32)
        tok_count = jnp.sum(weight)
        tgt = (labels[0] - shard_idx * shard_vocab)[None, :]
        bias = jnp.broadcast_to(jnp.where(valid_blk > 0, 0.0, -jnp.inf)[:, None], (shard_vocab, 128))
        z, m8, s8, p8 = forward(embed_blk, bias, x_all, tgt)
        m1 = jnp.max(m8, axis=0)
        part = jnp.stack([m1, jnp.sum(s8 * jnp.exp2(m8 - m1), axis=0), jnp.sum(p8, axis=0)])
        parts = lax.all_gather(part, "tp", axis=0)
        row_max = jnp.max(parts[:, 0], axis=0)
        lse2 = row_max + jnp.log2(jnp.sum(parts[:, 1] * jnp.exp2(parts[:, 0] - row_max), axis=0))
        tok_loss = (lse2 - jnp.sum(parts[:, 2], axis=0)) * LN2 * weight
        mean_loss = (jnp.sum(tok_loss) / tok_count).reshape(1)
        shift = jnp.where(weight > 0, lse2 + jnp.log2(tok_count), jnp.inf)[None, :]
        scale = (weight / tok_count)[None, :]
        dx_part = token_grad(embed_blk.T, shift, scale, tgt, z)
        dx_local = lax.psum_scatter(dx_part, "tp", scatter_dimension=0, tiled=False)
        d_embed = embed_grad(z, x_all, shift, scale, tgt, shard_vocab)
        d_hidden, ln_part = norm_grad(hidden_blk, ln_gamma, dx_local)
        ln_grads = lax.psum(ln_part, "tp")
        loss_local = lax.dynamic_slice_in_dim(tok_loss, shard_idx * tok_local, tok_local)
        return loss_local, mean_loss, d_hidden, d_embed, ln_grads[0], ln_grads[1]

    return jax.shard_map(local_step, mesh=mesh, in_specs=(row_spec, P(), P(), P("tp", None), P("tp"), tok_spec, tok_spec), out_specs=(tok_spec, P("dp"), row_spec, row_spec, P("dp"), P("dp")), check_vma=False)
```

time: 394 us -> 313 us (0.79)
  Pallas kernels: 0 us -> 212 us
  matrix products: 155 us -> 0 us
  other arithmetic: 105 us -> 10.8 us
  blocking collectives: 72.4 us -> 40.5 us
  waiting for transfers between devices: 42.7 us -> 11.6 us
  local copies, waits for them, and re-layouts: 2.5 us -> 19.4 us
    pallas_call x0 -> x4, Pallas kernels: none -> 212 us  [the longest x1 72.4 us: embed_grad(): pl.pallas_call(de_kernel, grid=(nv, t // TT), out_shape=jax.ShapeDtypeStr...]
    dot_general x3 -> x0, matrix products: 155 us -> none  [the longest x1 52.9 us: local_step(): lax.dot_general(x_all, embed_blk, (((1,), (1,)), ((), ())), preferred_ele...]
    convert_element_type x2 -> x0, other arithmetic: 52.6 us -> none  [the longest x1 51.6 us: local_step(): ((soft_probs - target_hit.astype(jnp.float32)) * (weight / tok_count)[:,...]
    reduce_sum x3, other arithmetic: 43.5 us -> 2.16 us  [the longest x1 1.03 us: local_step(): jnp.sum(s8 * jnp.exp2(m8 - m1), axis=0)]
    psum x2 -> x1, blocking collectives: 36.8 us -> 12.2 us  [local_step(): ln_grads = lax.psum(ln_part, 'tp')]
    pmax x1 -> x0, blocking collectives: 20.8 us -> none  [local_step(): row_max = lax.pmax(local_max, 'tp')]
    reduce_scatter x1, waiting for transfers between devices: 17.4 us -> 0.01 us  [local_step(): dx_local = lax.psum_scatter(dx_part, 'tp', scatter_dimension=0, tiled=False)]
    all_gather x1, waiting for transfers between devices: 25.2 us -> 11.5 us  [local_step(): lax.all_gather(normed.astype(jnp.bfloat16), 'tp', axis=0, tiled=True)]
  transfers between devices with their start and end apart: 2 -> 2, of which waited for: 2 -> 1; matrix products, arithmetic and copies ran while one was open for 14% -> 5% of each run, Pallas kernels for 0% -> 23%
where the time goes in v1:
time: 313 us; the launch traced here: 312 us
  Pallas kernels  212 us (68%)
  blocking collectives  40.5 us (13%)
  local copies, waits for them, and re-layouts  19.4 us (6%)
  between operations  17.4 us (6%)
  waiting for transfers between devices  11.6 us (4%)
  other arithmetic  10.8 us (3%)
    pallas_call x1, Pallas kernels, embed_grad(): pl.pallas_call(de_kernel, grid=(nv, t // TT), out_shape=jax.ShapeDtypeStr...  72.4 us
    pallas_call x1, Pallas kernels, token_grad(): pl.pallas_call(dx_kernel, out_shape=jax.ShapeDtypeStruct((t // TT, d, TT)...  70.9 us
    pallas_call x1, Pallas kernels, forward(): pl.pallas_call(forward_kernel, out_shape=(jax.ShapeDtypeStruct((nv * (t /...  64.4 us
    all_gather x1, blocking collectives, local_step(): lax.all_gather(jnp.stack([tgt_blk, mask_blk]), 'tp', axis=1, tiled=True)  14.8 us
    unnamed x13, local copies, waits for them, and re-layouts  13.8 us
    all_gather x1, blocking collectives, local_step(): parts = lax.all_gather(part, 'tp', axis=0)  13.5 us
    psum x1, blocking collectives, local_step(): ln_grads = lax.psum(ln_part, 'tp')  12.2 us
    all_gather x1, waiting for transfers between devices, local_step(): lax.all_gather(normed.astype(jnp.bfloat16), 'tp', axis=0, tiled=True)  11.5 us
  transfers between devices with their start and end apart: 2, of which 1 were waited for; matrix products, arithmetic and copies ran while one was open for 5% of the time, Pallas kernels for 23%

profile of v1, /device:TPU:81, one launch (start us, length us, event | category | flops | bytes accessed | tf_op | source)
XLA Modules:
  0.0 311.6 jit_solution(16767418546500517394)
XLA Ops:
  7.2 0.0 copy-start
  7.2 0.1 all-gather.4.cloned.1.call-start
  7.3 1.4 convert_reduce_fusion
  8.7 0.0 copy-start.4
  8.7 0.0 copy-start.5
  8.7 1.5 fusion.2
  10.2 1.2 fusion.5
  11.5 0.1 all-gather.4.cloned.1.call-update
  11.5 0.1 reduce-scatter.2.cloned.1.call-start
  11.6 14.8 %all_gather.13 = s32[2,4096]{1,0:T(2,128)S(1)} all-gather(s32[2,512]{1,0:T(2,128)S(1)} %pad_add_fusion), channel_id=1, replica_groups=mesh['dp'=4,'tp'=8] {'tp'}, dimensions={1}, use_global_device_ids=true | all-gather | bytes 36864 | tf_op jit(solution)/shard_map/all_gather | solution.py:250
  26.5 0.6 fusion.11
  27.8 13.8 %copy.16 = bf16[6400,768]{0,1:T(8,128)(2,1)} copy(bf16[6400,768]{1,0:T(8,128)(2,1)} %e_ref.1) | data formatting | bytes 19660800 | tf_op args[3]
  41.6 0.6 slice_subtract_fusion
  42.2 11.5 %all-gather.4.cloned.1.call-done.x_ref = bf16[4096,768]{1,0:T(8,128)(2,1)} async-done(((bf16[512,768]{1,0:T(8,128)(2,1)}), bf16[4096,768]{1,0:T(8,128)(2,1)}) %all-gather.4.cloned.1.call-update) | async-done | bytes 6291472 | tf_op jit(solution)/shard_map/all_gather | solution.py:249
  53.7 3.8 %broadcast_in_dim.18.bias_ref = f32[6400,128]{1,0:T(8,128)} broadcast(f32[6400]{0:T(1024)S(1)} %compare_select_fusion.1), dimensions={0} | broadcast | bytes 3302400 | tf_op jit(solution)/shard_map/broadcast_in_dim | solution.py:254
  57.5 64.4 %logits.1 = (f32[40,1280,512]{2,1,0:T(8,128)}, f32[8,4096]{1,0:T(8,128)}, f32[8,4096]{1,0:T(8,128)}, f32[8,4096]{1,0:T(8,128)}) custom-call(bf16[6400,768]{1,0:T(8,128)(2,1)} %e_ref.1, f32[6400,128]{1,0:T(8,128)} %broadcast_in_dim.18.bias_ref, bf16[4096,768]{1,0:T(8,128)(2,1)} %all-gather.4.cloned.1.call-done.x_ref, s32[1,4096]{1,0:T(1,128)} %get-tuple-element.31.tgt_ref), custom_call_target="tpu_custom_call" | custom-call | flops 40265318400 | bytes 104857600 | tf_op jit(solution)/shard_map/logits/pallas_call | solution.py:89
  121.9 0.9 reduce_sum.75
  122.9 0.9 reduce_max.18
  123.8 1.0 multiply_reduce_fusion
  124.9 13.5 %all-gather.1 = f32[8,3,4096]{2,1,0:T(4,128)S(1)} all-gather(f32[1,3,4096]{2,1,0:T(4,128)S(1)} %maximum_bitcast_fusion), channel_id=2, replica_groups=mesh['dp'=4,'tp'=8] {'tp'}, dimensions={0}, use_global_device_ids=true | all-gather | bytes 442368 | tf_op jit(solution)/shard_map/all_gather | solution.py:258
  138.4 0.4 fusion.13
  138.8 0.2 fusion.7
  139.0 0.6 fusion.12
  139.6 1.3 broadcast_divide_fusion
  140.9 70.9 %token_grad.1 = f32[8,768,512]{2,1,0:T(8,128)} custom-call(bf16[768,6400]{1,0:T(8,128)(2,1)} %bitcast.28, f32[1,4096]{1,0:T(1,128)} %get-tuple-element.29.lse_ref, f32[1,4096]{1,0:T(1,128)} %get-tuple-element.28.w_ref, s32[1,4096]{1,0:T(1,128)} %get-tuple-element.31.tgt_ref, f32[40,1280,512]{2,1,0:T(8,128)} %get-tuple-element.15.z_hbm.z_ref), custom_call_target="tpu_custom_call" | custom-call | flops 40265318400 | bytes 104857600 | tf_op jit(solution)/shard_map/token_grad/pallas_call | solution.py:167
  211.8 0.1 reduce-scatter.2.cloned.1.call-update
  211.9 0.6 broadcast_in_dim.19.gamma_ref
  213.8 0.7 dynamic_slice.3
  214.4 72.4 %embed_grad.1 = f32[6400,768]{1,0:T(8,128)} custom-call(f32[40,1280,512]{2,1,0:T(8,128)} %get-tuple-element.15.z_hbm.z_ref, bf16[4096,768]{1,0:T(8,128)(2,1)} %all-gather.4.cloned.1.call-done.x_ref, f32[1,4096]{1,0:T(1,128)} %get-tuple-element.29.lse_ref, f32[1,4096]{1,0:T(1,128)} %get-tuple-element.28.w_ref, s32[1,4096]{1,0:T(1,128)} %get-tuple-element.31.tgt_ref), custom_call_target="tpu_custom_call" | custom-call | flops 40265318400 | bytes 124518400 | tf_op jit(solution)/shard_map/embed_grad/pallas_call | solution.py:202
  286.9 3.9 %norm_grad.1 = (bf16[512,768]{1,0:T(8,128)(2,1)}, f32[2,768]{1,0:T(2,128)}) custom-call(bf16[512,768]{1,0:T(8,128)(2,1)} %h_ref.1, f32[1,768]{1,0:T(1,128)} %broadcast_in_dim.19.gamma_ref, f32[768,512]{1,0:T(8,128)} %bitcast.29), custom_call_target="tpu_custom_call" | custom-call | tf_op jit(solution)/shard_map/norm_grad/pallas_call | solution.py:230
  290.8 12.2 %psum.7 = f32[2,768]{1,0:T(2,128)S(1)} all-reduce(f32[2,768]{1,0:T(2,128)} %get-tuple-element.17), channel_id=1, replica_groups=mesh['dp'=4,'tp'=8] {'tp'}, use_global_device_ids=true, to_apply=%region_11.12 | all-reduce | flops 1536 | bytes 12288 | tf_op jit(solution)/shard_map/psum | solution.py:269
  303.0 0.6 slice_reduce_fusion.1
  (15 shorter events, 0.1 us)
Async XLA Ops:
  7.2 3.0 copy-start
  7.2 3.0 copy-start.3
  7.2 3.0 copy-start.2
  7.2 46.5 %all-gather.4.cloned.1.call-start = ((), (), s32[]{:S(2)}) async-start(), calls=%async_computation.1 | async-start | bytes 7077888 | tf_op jit(solution)/shard_map/all_gather | solution.py:249
  8.7 2.9 copy-start.4
  8.7 2.9 copy-start.5
  11.5 275.4 %reduce-scatter.2.cloned.1.call-start = ((), (), s32[]{:S(2)}) async-start(), calls=%async_computation.2 | async-start | bytes 14155776 | tf_op jit(solution)/shard_map/reduce_scatter | solution.py:266
  27.8 13.8 %copy-start.1 = (s32[6400]{0:T(1024)S(1)}, s32[6400]{0:T(1024)}, u32[]{:S(2)}) copy-start(s32[6400]{0:T(1024)} %param.11) | copy-start | bytes 76804
Sparse Core Ops, SparseCore 0:
  11.6 42.0 all-gather.3
  212.0 68.1 reduce-scatter.1

commit v2 on v1

--- a/solution.py
+++ b/solution.py
@@ -48,24 +48,44 @@
     p_ref[:, at] = picked
 
 
-def forward_kernel(e_ref, bias_ref, x_ref, tgt_ref, z_hbm, m_ref, s_ref, p_ref, *rest):
-    nv, nt = e_ref.shape[0] // TV, x_ref.shape[0] // TT
-    zb, out_sem = rest[:nv], rest[nv]
+def forward_kernel(e_hbm, keep_ref, x_hbm, tgt_ref, z_hbm, m_ref, s_ref, p_ref, e_ref, x_ref, bias_ref, *rest):
+    nv, nt = e_ref.shape[0] // TV, x_ref.shape[0]
+    zb, (out_sem, e_sem, x_sem) = rest[:nv], rest[nv:]
+
+    def load_e(v):
+        at = pl.ds(v * TV, TV)
+        return pltpu.make_async_copy(e_hbm.at[at], e_ref.at[at], e_sem.at[v])
+
+    def load_x(t):
+        return pltpu.make_async_copy(x_hbm.at[t, pl.ds(0, TT)], x_ref.at[t], x_sem.at[t])
+
+    load_x(0).start()
+    for v in range(nv):
+        load_e(v).start()
+    for t in range(1, nt):
+        load_x(t).start()
     m_ref[...] = jnp.full(m_ref.shape, LOW, jnp.float32)
     s_ref[...] = jnp.zeros(s_ref.shape, jnp.float32)
     p_ref[...] = jnp.zeros(p_ref.shape, jnp.float32)
     zb[-1][...] = jnp.full(zb[-1].shape, -jnp.inf, jnp.float32)
+    for j in range(keep_ref.shape[0]):
+        bias_ref[j * 128:(j + 1) * 128, :] = jnp.broadcast_to(keep_ref[j:j + 1, :], (128, 128)).T
 
     def out(k, t):
         return pltpu.make_async_copy(zb[k], z_hbm.at[t * nv + k], out_sem.at[k])
 
-    for k in range(nv):
-        out(k, 0).start()
-
     def body(t, carry):
-        x_blk = x_ref[pl.ds(pl.multiple_of(t * TT, TT), TT), :]
+        load_x(t).wait()
+        x_blk = x_ref[t]
         for v in range(nv):
-            out(v, 0).wait()
+            @pl.when(t == 0)
+            def _():
+                load_e(v).wait()
+
+            @pl.when(t > 0)
+            def _():
+                out(v, 0).wait()
+
             at = slice(v * TV, (v + 1) * TV)
             z = lax.dot_general(e_ref[at, :], x_blk, (((1,), (1,)), ((), ())), preferred_element_type=jnp.float32)
             zb[v][...] = z * LOG2E + jnp.concatenate([bias_ref[at, :]] * (TT // 128), axis=1)
@@ -82,20 +102,26 @@
         out(k, 0).wait()
 
 
-def forward(embed, bias, x_all, tgt):
-    v, t, d = embed.shape[0], x_all.shape[0], x_all.shape[1]
-    nv = v // TV
+def forward(embed, keep, x_all, tgt):
+    (v, d), nt = embed.shape, x_all.shape[0]
+    t, nv = nt * TT, v // TV
     stat = jax.ShapeDtypeStruct((8, t), jnp.float32)
     return pl.pallas_call(
         forward_kernel,
-        out_shape=(jax.ShapeDtypeStruct((nv * (t // TT), TV, TT), jnp.float32), stat, stat, stat),
-        in_specs=[VM] * 4,
+        out_shape=(jax.ShapeDtypeStruct((nv * nt, TV, TT), jnp.float32), stat, stat, stat),
+        in_specs=[ANY, VM, ANY, VM],
         out_specs=(ANY, VM, VM, VM),
-        scratch_shapes=[pltpu.VMEM((TV, TT), jnp.float32)] * nv + [pltpu.SemaphoreType.DMA((nv,))],
+        scratch_shapes=[
+            pltpu.VMEM((v, d), jnp.bfloat16),
+            pltpu.VMEM((nt, TT, d), jnp.bfloat16),
+            pltpu.VMEM((v, 128), jnp.float32),
+        ]
+        + [pltpu.VMEM((TV, TT), jnp.float32)] * nv
+        + [pltpu.SemaphoreType.DMA((nv,)), pltpu.SemaphoreType.DMA((nv,)), pltpu.SemaphoreType.DMA((nt,))],
         compiler_params=pltpu.CompilerParams(vmem_limit_bytes=VMEM_LIMIT),
         cost_estimate=pl.CostEstimate(flops=2 * v * t * d, bytes_accessed=4 * v * t, transcendentals=v * t),
         name="logits",
-    )(embed, bias, x_all, tgt)
+    )(embed, keep, x_all, tgt)
 
 
 def tile_grad(z_ref, dz_ref, base, col, lse_ref, w_ref, tgt_ref):
@@ -178,33 +204,70 @@
     )(embed_t, lse, w, tgt, z)
 
 
-def de_kernel(z_ref, x_ref, lse_ref, w_ref, tgt_ref, o_ref):
-    v, t = pl.program_id(0), pl.program_id(1)
-    at = cols(t * TT)
-    lse = lse_ref[:, at]
-    w = jnp.broadcast_to(w_ref[:, at], (8, TT))
-    rel = jnp.broadcast_to(tgt_ref[:, at], (8, TT)) - lax.broadcasted_iota(jnp.int32, (8, TT), 0) - v * TV
-    x_blk = x_ref[pl.ds(pl.multiple_of(t * TT, TT), TT), :]
-
-    @pl.when(t == 0)
-    def _():
-        o_ref[...] = jnp.zeros_like(o_ref)
-
-    for k in range(0, TV, 256):
-        p = jnp.exp2(z_ref[0, k:k + 256] - lse)
-        dz = jnp.concatenate([p[r:r + 8] - jnp.where(rel == k + r, w, 0.0) for r in range(0, 256, 8)], axis=0)
-        o_ref[k:k + 256] += jnp.dot(dz.astype(jnp.bfloat16), x_blk, preferred_element_type=jnp.float32)
+def de_kernel(z_hbm, x_ref, lse_ref, w_ref, tgt_ref, o_hbm, acc, *rest):
+    nt = x_ref.shape[0]
+    nv = z_hbm.shape[0] // nt
+    zb, (z_sem, o_sem) = rest[:4], rest[4:]
+
+    def z_in(k, g):
+        v, t = lax.div(g, nt // 4), lax.rem(g, nt // 4) * 4 + k
+        return pltpu.make_async_copy(z_hbm.at[t * nv + v], zb[k], z_sem.at[k])
+
+    def o_out(v):
+        return pltpu.make_async_copy(acc.at[lax.rem(v, 2)], o_hbm.at[pl.ds(pl.multiple_of(v * TV, TV), TV)], o_sem.at[lax.rem(v, 2)])
+
+    for k in range(4):
+        z_in(k, 0).start()
+    last = nv * (nt // 4) - 1
+
+    def body(g, carry):
+        v, q = lax.div(g, nt // 4), lax.rem(g, nt // 4)
+        slot = lax.rem(v, 2)
+
+        @pl.when((q == 0) & (v >= 2))
+        def _():
+            o_out(v).wait()
+
+        for k in range(4):
+            z_in(k, 0).wait()
+            t = q * 4 + k
+            at = cols(t * TT)
+            lse = lse_ref[:, at]
+            w = jnp.broadcast_to(w_ref[:, at], (8, TT))
+            rel = jnp.broadcast_to(tgt_ref[:, at], (8, TT)) - lax.broadcasted_iota(jnp.int32, (8, TT), 0) - v * TV
+            x_blk = x_ref[t, :TT]
+            for c in range(0, TV, 256):
+                p = jnp.exp2(zb[k][c:c + 256] - lse)
+                dz = jnp.concatenate([p[r:r + 8] - jnp.where(rel == c + r, w, 0.0) for r in range(0, 256, 8)], axis=0)
+                d = jnp.dot(dz.astype(jnp.bfloat16), x_blk, preferred_element_type=jnp.float32)
+                old = acc[slot, c:c + 256]
+                acc[slot, c:c + 256] = d + (jnp.where(q == 0, 0.0, old) if k == 0 else old)
+            z_in(k, jnp.minimum(g + 1, last)).start()
+
+        @pl.when(q == nt // 4 - 1)
+        def _():
+            o_out(v).start()
+
+        return carry
+
+    lax.fori_loop(0, last + 1, body, 0)
+    for k in range(4):
+        z_in(k, 0).wait()
+    for v in range(max(nv - 2, 0), nv):
+        o_out(v).wait()
 
 
 def embed_grad(z, x_all, lse, w, tgt, v):
-    t, d = x_all.shape
-    nv = v // TV
+    nt, _, d = x_all.shape
+    t = nt * TT
     return pl.pallas_call(
         de_kernel,
-        grid=(nv, t // TT),
         out_shape=jax.ShapeDtypeStruct((v, d), jnp.float32),
-        in_specs=[pl.BlockSpec((1, TV, TT), lambda i, j: (j * nv + i, 0, 0))] + [VM] * 4,
-        out_specs=pl.BlockSpec((TV, d), lambda i, j: (i, 0)),
+        in_specs=[ANY] + [VM] * 4,
+        out_specs=ANY,
+        scratch_shapes=[pltpu.VMEM((2, TV, d), jnp.float32)]
+        + [pltpu.VMEM((TV, TT), jnp.float32)] * 4
+        + [pltpu.SemaphoreType.DMA((4,)), pltpu.SemaphoreType.DMA((2,))],
         compiler_params=pltpu.CompilerParams(vmem_limit_bytes=VMEM_LIMIT),
         cost_estimate=pl.CostEstimate(flops=2 * v * t * d, bytes_accessed=4 * v * t + 4 * v * d, transcendentals=v * t),
         name="embed_grad",
@@ -246,13 +309,17 @@
         shard_vocab = embed_blk.shape[0]
         shard_idx = lax.axis_index("tp")
         normed = layer_norm(hidden_blk.astype(jnp.float32), ln_gamma, ln_beta)
-        x_all = lax.all_gather(normed.astype(jnp.bfloat16), "tp", axis=0, tiled=True)
-        labels = lax.all_gather(jnp.stack([tgt_blk, mask_blk]), "tp", axis=1, tiled=True)
-        weight = labels[1].astype(jnp.float32)
+        label_rows = jnp.stack([tgt_blk // 256, tgt_blk % 256, mask_blk]).astype(jnp.bfloat16)
+        label_rows = jnp.pad(label_rows, ((0, 16 - label_rows.shape[0]), (0, hidden_blk.shape[1] - tok_local)))
+        packed = jnp.concatenate([normed.astype(jnp.bfloat16), label_rows], axis=0)
+        x_all = lax.all_gather(packed, "tp", axis=0)
+        labels = x_all[:, tok_local:tok_local + 3, :tok_local].astype(jnp.float32)
+        weight = labels[:, 2].reshape(-1)
         tok_count = jnp.sum(weight)
-        tgt = (labels[0] - shard_idx * shard_vocab)[None, :]
-        bias = jnp.broadcast_to(jnp.where(valid_blk > 0, 0.0, -jnp.inf)[:, None], (shard_vocab, 128))
-        z, m8, s8, p8 = forward(embed_blk, bias, x_all, tgt)
+        target_ids = (labels[:, 0] * 256.0 + labels[:, 1]).astype(jnp.int32).reshape(-1)
+        tgt = (target_ids - shard_idx * shard_vocab)[None, :]
+        keep = jnp.where(valid_blk > 0, 0.0, -jnp.inf).reshape(-1, 128)
+        z, m8, s8, p8 = forward(embed_blk, keep, x_all, tgt)
         m1 = jnp.max(m8, axis=0)
         part = jnp.stack([m1, jnp.sum(s8 * jnp.exp2(m8 - m1), axis=0), jnp.sum(p8, axis=0)])
         parts = lax.all_gather(part, "tp", axis=0)

time: 313 us -> 303 us (0.968)
  waiting for transfers between devices: 11.6 us -> 34.1 us
  Pallas kernels: 212 us -> 195 us
  blocking collectives: 40.5 us -> 26.6 us
  local copies, waits for them, and re-layouts: 19.4 us -> 15 us
  other arithmetic: 10.8 us -> 14.5 us
    pallas_call x2, Pallas kernels: 137 us -> 120 us  [the longest x1 60.2 us: embed_grad(): pl.pallas_call(de_kernel, out_shape=jax.ShapeDtypeStruct((v, d), jnp.floa...]
    all_gather x1, waiting for transfers between devices: 11.5 us -> 28.6 us  [local_step(): x_all = lax.all_gather(packed, 'tp', axis=0)]
    all_gather x1 -> x0, blocking collectives: 14.8 us -> none  [local_step(): lax.all_gather(jnp.stack([tgt_blk, mask_blk]), 'tp', axis=1, tiled=True)]
    reduce_scatter x1, waiting for transfers between devices: 0.01 us -> 5.43 us  [local_step(): dx_local = lax.psum_scatter(dx_part, 'tp', scatter_dimension=0, tiled=False)]
    broadcast_in_dim x1 -> x0, local copies, waits for them, and re-layouts: 3.79 us -> none  [local_step(): jnp.broadcast_to(jnp.where(valid_blk > 0, 0.0, -jnp.inf)[:, None], (shard...]
    unnamed x13 -> x9, local copies, waits for them, and re-layouts: 13.8 us -> 13.8 us
  transfers between devices with their start and end apart: 2 -> 2, of which waited for: 1 -> 2; matrix products, arithmetic and copies ran while one was open for 5% -> 5% of each run, Pallas kernels for 23% -> 20%
where the time goes in v2:
time: 303 us; the launch traced here: 302 us
  Pallas kernels  195 us (64%)
  waiting for transfers between devices  34.1 us (11%)
  blocking collectives  26.6 us (9%)
  between operations  17.4 us (6%)
  local copies, waits for them, and re-layouts  15 us (5%)
  other arithmetic  14.5 us (5%)
    pallas_call x1, Pallas kernels, token_grad(): pl.pallas_call(dx_kernel, out_shape=jax.ShapeDtypeStruct((t // TT, d, TT)...  71 us
    pallas_call x1, Pallas kernels, embed_grad(): pl.pallas_call(de_kernel, out_shape=jax.ShapeDtypeStruct((v, d), jnp.floa...  60.2 us
    pallas_call x1, Pallas kernels, forward(): pl.pallas_call(forward_kernel, out_shape=(jax.ShapeDtypeStruct((nv * nt,...  59.5 us
    all_gather x1, waiting for transfers between devices, local_step(): x_all = lax.all_gather(packed, 'tp', axis=0)  28.6 us
    unnamed x9, local copies, waits for them, and re-layouts  13.8 us
    all_gather x1, blocking collectives, local_step(): parts = lax.all_gather(part, 'tp', axis=0)  13.5 us
    psum x1, blocking collectives, local_step(): ln_grads = lax.psum(ln_part, 'tp')  13.1 us
  transfers between devices with their start and end apart: 2, of which 2 were waited for; matrix products, arithmetic and copies ran while one was open for 5% of the time, Pallas kernels for 20%

profile of v2, /device:TPU:81, one launch (start us, length us, event | category | flops | bytes accessed | tf_op | source)
XLA Modules:
  0.0 302.3 jit_solution(17159660881886448120)
XLA Ops:
  7.2 0.1 all-gather.5.cloned.1.call-start
  7.3 0.7 convert.14
  8.0 0.7 fusion.22
  8.7 1.3 convert_reduce_fusion
  10.1 1.5 fusion.2
  11.6 0.4 fusion.5
  12.0 0.9 pad_maximum_fusion
  13.0 0.1 reduce-scatter.2.cloned.1.call-start
  13.1 13.8 %copy.16 = bf16[6400,768]{0,1:T(8,128)(2,1)} copy(bf16[6400,768]{1,0:T(8,128)(2,1)} %e_hbm.1) | data formatting | bytes 19660800 | tf_op args[3]
  26.8 0.6 select_bitcast_fusion.keep_ref
  27.4 28.6 %all-gather.5.cloned.1.call-done = bf16[4224,768]{1,0:T(8,128)(2,1)} async-done(((bf16[528,768]{1,0:T(8,128)(2,1)}), bf16[4224,768]{1,0:T(8,128)(2,1)}) %all-gather.5.cloned.1.call-update) | async-done | bytes 6488080 | tf_op jit(solution)/shard_map/all_gather | solution.py:315
  56.0 0.8 slice_convert_fusion
  56.9 0.6 fusion.21
  57.6 59.5 %logits.1 = (f32[40,1280,512]{2,1,0:T(8,128)}, f32[8,4096]{1,0:T(8,128)}, f32[8,4096]{1,0:T(8,128)}, f32[8,4096]{1,0:T(8,128)}) custom-call(bf16[6400,768]{1,0:T(8,128)(2,1)} %e_hbm.1, f32[50,128]{1,0:T(8,128)} %select_bitcast_fusion.keep_ref, bf16[8,528,768]{2,1,0:T(8,128)(2,1)} %bitcast.48, s32[1,4096]{1,0:T(1,128)} %bitcast.42), custom_call_target="tpu_custom_call" | custom-call | flops 40265318400 | bytes 104857600 | tf_op jit(solution)/shard_map/logits/pallas_call | solution.py:109
  117.1 0.9 reduce_sum.75
  118.0 0.9 reduce_max.18
  119.0 1.0 multiply_reduce_fusion
  120.1 13.5 %all-gather.2 = f32[8,3,4096]{2,1,0:T(4,128)S(1)} all-gather(f32[1,3,4096]{2,1,0:T(4,128)S(1)} %maximum_bitcast_fusion), channel_id=3, replica_groups=mesh['dp'=4,'tp'=8] {'tp'}, dimensions={0}, use_global_device_ids=true | all-gather | bytes 442368 | tf_op jit(solution)/shard_map/all_gather | solution.py:325
  133.5 0.4 fusion.25
  133.9 0.2 fusion.7
  134.1 0.6 slice_reduce_fusion.3
  134.8 1.3 broadcast_divide_fusion
  136.8 0.6 broadcast_select_fusion.lse_ref
  137.4 71.0 %token_grad.1 = f32[8,768,512]{2,1,0:T(8,128)} custom-call(bf16[768,6400]{1,0:T(8,128)(2,1)} %bitcast.33, f32[1,4096]{1,0:T(1,128)} %broadcast_select_fusion.lse_ref, f32[1,4096]{1,0:T(1,128)} %bitcast.45, s32[1,4096]{1,0:T(1,128)} %bitcast.43, f32[40,1280,512]{2,1,0:T(8,128)} %get-tuple-element.15.z_hbm), custom_call_target="tpu_custom_call" | custom-call | flops 40265318400 | bytes 104857600 | tf_op jit(solution)/shard_map/token_grad/pallas_call | solution.py:193
  208.4 0.1 reduce-scatter.2.cloned.1.call-update
  208.4 0.6 broadcast_in_dim.26.gamma_ref
  210.4 0.7 dynamic-slice_multiply_fusion
  211.0 60.2 %embed_grad.1 = f32[6400,768]{1,0:T(8,128)} custom-call(f32[40,1280,512]{2,1,0:T(8,128)} %get-tuple-element.15.z_hbm, bf16[8,528,768]{2,1,0:T(8,128)(2,1)} %bitcast.49, f32[1,4096]{1,0:T(1,128)} %broadcast_select_fusion.lse_ref, f32[1,4096]{1,0:T(1,128)} %bitcast.46, s32[1,4096]{1,0:T(1,128)} %bitcast.44), custom_call_target="tpu_custom_call" | custom-call | flops 40265318400 | bytes 124518400 | tf_op jit(solution)/shard_map/embed_grad/pallas_call | solution.py:263
  271.3 5.4 %reduce-scatter.2.cloned.1.call-done = f32[1,768,512]{2,1,0:T(8,128)} async-done(((f32[8,768,512]{2,1,0:T(8,128)}), f32[1,768,512]{2,1,0:T(8,128)}) %reduce-scatter.2.cloned.1.call-update) | async-done | bytes 1572880 | tf_op jit(solution)/shard_map/reduce_scatter | solution.py:333
  276.7 3.9 %norm_grad.1 = (bf16[512,768]{1,0:T(8,128)(2,1)}, f32[2,768]{1,0:T(2,128)}) custom-call(bf16[512,768]{1,0:T(8,128)(2,1)} %h_ref.1, f32[1,768]{1,0:T(1,128)} %broadcast_in_dim.26.gamma_ref, f32[768,512]{1,0:T(8,128)} %bitcast.34), custom_call_target="tpu_custom_call" | custom-call | tf_op jit(solution)/shard_map/norm_grad/pallas_call | solution.py:293
  280.6 13.1 %psum.7 = f32[2,768]{1,0:T(2,128)S(1)} all-reduce(f32[2,768]{1,0:T(2,128)} %get-tuple-element.17), channel_id=1, replica_groups=mesh['dp'=4,'tp'=8] {'tp'}, use_global_device_ids=true, to_apply=%region_11.12 | all-reduce | flops 1536 | bytes 12288 | tf_op jit(solution)/shard_map/psum | solution.py:336
  293.7 0.6 slice_reduce_fusion.1
  (19 shorter events, 0.2 us)
Async XLA Ops:
  7.2 4.4 %copy-start = (bf16[512,768]{1,0:T(8,128)(2,1)S(1)}, bf16[512,768]{1,0:T(8,128)(2,1)}, u32[]{:S(2)}) copy-start(bf16[512,768]{1,0:T(8,128)(2,1)} %h_ref.1) | copy-start | bytes 2359300
  7.2 4.4 %copy-start.3 = (f32[768]{0:T(1024)S(1)}, f32[768]{0:T(1024)}, u32[]{:S(2)}) copy-start(f32[768]{0:T(1024)} %param.9) | copy-start | bytes 9220
  7.2 4.4 %copy-start.2 = (f32[768]{0:T(1024)S(1)}, f32[768]{0:T(1024)}, u32[]{:S(2)}) copy-start(f32[768]{0:T(1024)} %param.8) | copy-start | bytes 9220
  7.2 48.8 %all-gather.5.cloned.1.call-start = ((), (), s32[]{:S(2)}) async-start(), calls=%async_computation.2 | async-start | bytes 7299072 | tf_op jit(solution)/shard_map/all_gather | solution.py:315
  13.0 263.7 %reduce-scatter.2.cloned.1.call-start = ((), (), s32[]{:S(2)}) async-start(), calls=%async_computation.1 | async-start | bytes 14155776 | tf_op jit(solution)/shard_map/reduce_scatter | solution.py:333
  13.1 13.8 %copy-start.1 = (s32[6400]{0:T(1024)S(1)}, s32[6400]{0:T(1024)}, u32[]{:S(2)}) copy-start(s32[6400]{0:T(1024)} %param.11) | copy-start | bytes 76804
Sparse Core Ops, SparseCore 0:
  13.1 42.8 all-gather.4
  208.6 68.0 reduce-scatter.1

commit v3 on v2

--- a/solution.py
+++ b/solution.py
@@ -274,28 +274,95 @@
     )(z, x_all, lse, w, tgt)
 
 
-def norm_grad_kernel(h_ref, gamma_ref, dxt_ref, dh_ref, g_ref):
+def exchange(slots, me, n, send_sem, recv_sem):
+    barrier = pltpu.get_barrier_semaphore()
+    peers = [lax.rem(me + k, n) for k in range(1, n)]
+    for peer in peers:
+        pl.semaphore_signal(barrier, inc=1, device_id={"tp": peer}, device_id_type=pl.DeviceIdType.MESH)
+    pl.semaphore_wait(barrier, n - 1)
+    copies = [
+        pltpu.make_async_remote_copy(
+            src_ref=slots.at[me],
+            dst_ref=slots.at[me],
+            send_sem=send_sem.at[k],
+            recv_sem=recv_sem.at[k],
+            device_id={"tp": peer},
+            device_id_type=pl.DeviceIdType.MESH,
+        )
+        for k, peer in enumerate(peers)
+    ]
+    for copy in copies:
+        copy.start()
+    for copy in copies:
+        copy.wait()
+
+
+def combine_kernel(n, m_ref, s_ref, p_ref, lse_ref, picked_ref, slots, send_sem, recv_sem):
+    me = lax.axis_index("tp")
+    m = m_ref[...]
+    top = jnp.max(m, axis=0, keepdims=True)
+    slots[me, 0:1, :] = top
+    slots[me, 1:2, :] = jnp.sum(s_ref[...] * jnp.exp2(m - top), axis=0, keepdims=True)
+    slots[me, 2:3, :] = jnp.sum(p_ref[...], axis=0, keepdims=True)
+    slots[me, 3:4, :] = jnp.zeros_like(top)
+    exchange(slots, me, n, send_sem, recv_sem)
+    row_max = slots[0, 0:1, :]
+    for i in range(1, n):
+        row_max = jnp.maximum(row_max, slots[i, 0:1, :])
+    total = jnp.zeros_like(row_max)
+    picked = jnp.zeros_like(row_max)
+    for i in range(n):
+        total = total + slots[i, 1:2, :] * jnp.exp2(slots[i, 0:1, :] - row_max)
+        picked = picked + slots[i, 2:3, :]
+    lse_ref[...] = row_max + jnp.log2(total)
+    picked_ref[...] = picked
+
+
+def combine(m8, s8, p8, n):
+    t = m8.shape[1]
+    row = jax.ShapeDtypeStruct((1, t), jnp.float32)
+    return pl.pallas_call(
+        functools.partial(combine_kernel, n),
+        out_shape=(row, row),
+        in_specs=[VM] * 3,
+        out_specs=(VM, VM),
+        scratch_shapes=[pltpu.VMEM((n, 4, t), jnp.float32), pltpu.SemaphoreType.DMA((n - 1,)), pltpu.SemaphoreType.DMA((n - 1,))],
+        compiler_params=pltpu.CompilerParams(collective_id=0, has_side_effects=True),
+        name="combine",
+    )(m8, s8, p8)
+
+
+def norm_grad_kernel(n, h_ref, gamma_ref, dxt_ref, dh_ref, g_ref, slots, send_sem, recv_sem):
+    me = lax.axis_index("tp")
     h = h_ref[...].astype(jnp.float32)
     mean = jnp.mean(h, axis=1, keepdims=True)
     cen = h - mean
     rstd = lax.rsqrt(jnp.mean(cen * cen, axis=1, keepdims=True) + LN_EPS)
     xhat = cen * rstd
     dy = dxt_ref[...].T
-    g_ref[0:1, :] = jnp.sum(dy * xhat, axis=0, keepdims=True)
-    g_ref[1:2, :] = jnp.sum(dy, axis=0, keepdims=True)
+    d = dy.shape[1]
+    slots[me, 0:1, :] = jnp.sum(dy * xhat, axis=0, keepdims=True)
+    slots[me, 1:2, :] = jnp.sum(dy, axis=0, keepdims=True)
+    slots[me, 2:8, :] = jnp.zeros((6, d), jnp.float32)
     dn = dy * gamma_ref[...]
     dh = rstd * (dn - jnp.mean(dn, axis=1, keepdims=True) - xhat * jnp.mean(dn * xhat, axis=1, keepdims=True))
     dh_ref[...] = dh.astype(jnp.bfloat16)
-
-
-def norm_grad(hidden, gamma, dx_t):
+    exchange(slots, me, n, send_sem, recv_sem)
+    total = slots[0]
+    for i in range(1, n):
+        total = total + slots[i]
+    g_ref[...] = total
+
+
+def norm_grad(hidden, gamma, dx_t, n):
     t, d = hidden.shape
     return pl.pallas_call(
-        norm_grad_kernel,
-        out_shape=(jax.ShapeDtypeStruct((t, d), jnp.bfloat16), jax.ShapeDtypeStruct((2, d), jnp.float32)),
+        functools.partial(norm_grad_kernel, n),
+        out_shape=(jax.ShapeDtypeStruct((t, d), jnp.bfloat16), jax.ShapeDtypeStruct((8, d), jnp.float32)),
         in_specs=[VM] * 3,
         out_specs=(VM, VM),
-        compiler_params=pltpu.CompilerParams(vmem_limit_bytes=VMEM_LIMIT),
+        scratch_shapes=[pltpu.VMEM((n, 8, d), jnp.float32), pltpu.SemaphoreType.DMA((n - 1,)), pltpu.SemaphoreType.DMA((n - 1,))],
+        compiler_params=pltpu.CompilerParams(collective_id=1, has_side_effects=True, vmem_limit_bytes=VMEM_LIMIT),
         name="norm_grad",
     )(hidden, gamma[None, :], dx_t)
 
@@ -303,6 +370,7 @@
 def solution(mesh):
     tok_spec = P(("dp", "tp"))
     row_spec = P(("dp", "tp"), None)
+    group = mesh.shape["tp"]
 
     def local_step(hidden_blk, ln_gamma, ln_beta, embed_blk, valid_blk, tgt_blk, mask_blk):
         tok_local = hidden_blk.shape[0]
@@ -320,20 +388,16 @@
         tgt = (target_ids - shard_idx * shard_vocab)[None, :]
         keep = jnp.where(valid_blk > 0, 0.0, -jnp.inf).reshape(-1, 128)
         z, m8, s8, p8 = forward(embed_blk, keep, x_all, tgt)
-        m1 = jnp.max(m8, axis=0)
-        part = jnp.stack([m1, jnp.sum(s8 * jnp.exp2(m8 - m1), axis=0), jnp.sum(p8, axis=0)])
-        parts = lax.all_gather(part, "tp", axis=0)
-        row_max = jnp.max(parts[:, 0], axis=0)
-        lse2 = row_max + jnp.log2(jnp.sum(parts[:, 1] * jnp.exp2(parts[:, 0] - row_max), axis=0))
-        tok_loss = (lse2 - jnp.sum(parts[:, 2], axis=0)) * LN2 * weight
+        lse2, picked = combine(m8, s8, p8, group)
+        lse2 = lse2[0]
+        tok_loss = (lse2 - picked[0]) * LN2 * weight
         mean_loss = (jnp.sum(tok_loss) / tok_count).reshape(1)
         shift = jnp.where(weight > 0, lse2 + jnp.log2(tok_count), jnp.inf)[None, :]
         scale = (weight / tok_count)[None, :]
         dx_part = token_grad(embed_blk.T, shift, scale, tgt, z)
         dx_local = lax.psum_scatter(dx_part, "tp", scatter_dimension=0, tiled=False)
         d_embed = embed_grad(z, x_all, shift, scale, tgt, shard_vocab)
-        d_hidden, ln_part = norm_grad(hidden_blk, ln_gamma, dx_local)
-        ln_grads = lax.psum(ln_part, "tp")
+        d_hidden, ln_grads = norm_grad(hidden_blk, ln_gamma, dx_local, group)
         loss_local = lax.dynamic_slice_in_dim(tok_loss, shard_idx * tok_local, tok_local)
         return loss_local, mean_loss, d_hidden, d_embed, ln_grads[0], ln_grads[1]
 

time: 303 us -> 297 us (0.980)
  blocking collectives: 26.6 us -> 0 us
  Pallas kernels: 195 us -> 214 us
    pallas_call x1 -> x2, Pallas kernels: 3.95 us -> 23.2 us  [the longest x1 12 us: combine(): pl.pallas_call(functools.partial(combine_kernel, n), out_shape=(row, row)...]
    all_gather x1 -> x0, blocking collectives: 13.5 us -> none  [local_step(): parts = lax.all_gather(part, 'tp', axis=0)]
    psum x1 -> x0, blocking collectives: 13.1 us -> none  [local_step(): ln_grads = lax.psum(ln_part, 'tp')]
    unnamed x9 -> x10, local copies, waits for them, and re-layouts: 13.8 us -> 15.8 us
where the time goes in v3:
time: 297 us; the launch traced here: 296 us
  Pallas kernels  214 us (72%)
  waiting for transfers between devices  34.6 us (12%)
  local copies, waits for them, and re-layouts  17.9 us (6%)
  between operations  17.4 us (6%)
  other arithmetic  12.4 us (4%)
    pallas_call x1, Pallas kernels, token_grad(): pl.pallas_call(dx_kernel, out_shape=jax.ShapeDtypeStruct((t // TT, d, TT)...  70.9 us
    pallas_call x1, Pallas kernels, embed_grad(): pl.pallas_call(de_kernel, out_shape=jax.ShapeDtypeStruct((v, d), jnp.floa...  60.2 us
    pallas_call x1, Pallas kernels, forward(): pl.pallas_call(forward_kernel, out_shape=(jax.ShapeDtypeStruct((nv * nt,...  59.7 us
    all_gather x1, waiting for transfers between devices, local_step(): x_all = lax.all_gather(packed, 'tp', axis=0)  28.6 us
    unnamed x10, local copies, waits for them, and re-layouts  15.8 us
    pallas_call x1, Pallas kernels, combine(): pl.pallas_call(functools.partial(combine_kernel, n), out_shape=(row, row)...  12 us
    pallas_call x1, Pallas kernels, norm_grad(): pl.pallas_call(functools.partial(norm_grad_kernel, n), out_shape=(jax.Sha...  11.2 us
  transfers between devices with their start and end apart: 2, of which 2 were waited for; matrix products, arithmetic and copies ran while one was open for 5% of the time, Pallas kernels for 20%

profile of v3, /device:TPU:81, one launch (start us, length us, event | category | flops | bytes accessed | tf_op | source)
XLA Modules:
  0.0 296.4 jit_solution(10504628145975102177)
XLA Ops:
  7.2 0.0 copy-start
  7.2 0.0 copy-start.3
  7.2 0.1 all-gather.3.cloned.1.call-start
  7.3 0.7 convert.14
  8.0 0.7 fusion.17
  8.7 1.3 convert_reduce_fusion
  10.1 1.5 fusion.2
  11.6 0.4 fusion.5
  12.0 0.9 pad_maximum_fusion
  12.9 0.1 all-gather.3.cloned.1.call-update
  13.0 0.1 reduce-scatter.2.cloned.1.call-start
  13.1 0.0 copy-start.1
  13.1 13.8 %copy.13 = bf16[6400,768]{0,1:T(8,128)(2,1)} copy(bf16[6400,768]{1,0:T(8,128)(2,1)} %e_hbm.1) | data formatting | bytes 19660800 | tf_op args[3]
  26.8 0.6 select_bitcast_fusion.keep_ref
  27.4 28.6 %all-gather.3.cloned.1.call-done = bf16[4224,768]{1,0:T(8,128)(2,1)} async-done(((bf16[528,768]{1,0:T(8,128)(2,1)}), bf16[4224,768]{1,0:T(8,128)(2,1)}) %all-gather.3.cloned.1.call-update) | async-done | bytes 6488080 | tf_op jit(solution)/shard_map/all_gather | solution.py:383
  56.0 0.8 slice_convert_fusion
  56.9 0.6 fusion.16
  57.5 59.7 %logits.1 = (f32[40,1280,512]{2,1,0:T(8,128)}, f32[8,4096]{1,0:T(8,128)}, f32[8,4096]{1,0:T(8,128)}, f32[8,4096]{1,0:T(8,128)}) custom-call(bf16[6400,768]{1,0:T(8,128)(2,1)} %e_hbm.1, f32[50,128]{1,0:T(8,128)} %select_bitcast_fusion.keep_ref, bf16[8,528,768]{2,1,0:T(8,128)(2,1)} %bitcast.24, s32[1,4096]{1,0:T(1,128)} %bitcast.18), custom_call_target="tpu_custom_call" | custom-call | flops 40265318400 | bytes 104857600 | tf_op jit(solution)/shard_map/logits/pallas_call | solution.py:109
  117.2 12.0 %combine.1 = (f32[1,4096]{1,0:T(1,128)}, f32[1,4096]{1,0:T(1,128)}) custom-call(f32[8,4096]{1,0:T(8,128)} %get-tuple-element.14.m_ref, f32[8,4096]{1,0:T(8,128)} %get-tuple-element.15.s_ref, f32[8,4096]{1,0:T(8,128)} %get-tuple-element.16.p_ref), custom_call_target="tpu_custom_call" | custom-call | tf_op jit(solution)/shard_map/combine/pallas_call | solution.py:324
  129.2 0.8 subtract_multiply_fusion
  130.0 0.6 slice_reduce_fusion.2
  130.6 1.3 broadcast_divide_fusion
  132.6 1.3 add_select_fusion.lse_ref
  133.9 70.9 %token_grad.1 = f32[8,768,512]{2,1,0:T(8,128)} custom-call(bf16[768,6400]{1,0:T(8,128)(2,1)} %bitcast.12, f32[1,4096]{1,0:T(1,128)} %add_select_fusion.lse_ref, f32[1,4096]{1,0:T(1,128)} %bitcast.21, s32[1,4096]{1,0:T(1,128)} %bitcast.19, f32[40,1280,512]{2,1,0:T(8,128)} %get-tuple-element.19.z_hbm), custom_call_target="tpu_custom_call" | custom-call | flops 40265318400 | bytes 104857600 | tf_op jit(solution)/shard_map/token_grad/pallas_call | solution.py:193
  204.9 0.1 reduce-scatter.2.cloned.1.call-update
  204.9 0.6 broadcast_in_dim.24.gamma_ref
  206.9 0.7 dynamic-slice_multiply_fusion
  207.5 60.2 %embed_grad.1 = f32[6400,768]{1,0:T(8,128)} custom-call(f32[40,1280,512]{2,1,0:T(8,128)} %get-tuple-element.19.z_hbm, bf16[8,528,768]{2,1,0:T(8,128)(2,1)} %bitcast.25, f32[1,4096]{1,0:T(1,128)} %add_select_fusion.lse_ref, f32[1,4096]{1,0:T(1,128)} %bitcast.22, s32[1,4096]{1,0:T(1,128)} %bitcast.20), custom_call_target="tpu_custom_call" | custom-call | flops 40265318400 | bytes 124518400 | tf_op jit(solution)/shard_map/embed_grad/pallas_call | solution.py:263
  267.7 5.9 %reduce-scatter.2.cloned.1.call-done = f32[1,768,512]{2,1,0:T(8,128)} async-done(((f32[8,768,512]{2,1,0:T(8,128)}), f32[1,768,512]{2,1,0:T(8,128)}) %reduce-scatter.2.cloned.1.call-update) | async-done | bytes 1572880 | tf_op jit(solution)/shard_map/reduce_scatter | solution.py:398
  273.7 11.2 %norm_grad.1 = (bf16[512,768]{1,0:T(8,128)(2,1)}, f32[8,768]{1,0:T(8,128)}) custom-call(bf16[512,768]{1,0:T(8,128)(2,1)} %h_ref.1, f32[1,768]{1,0:T(1,128)} %broadcast_in_dim.24.gamma_ref, f32[768,512]{1,0:T(8,128)} %bitcast.13), custom_call_target="tpu_custom_call" | custom-call | tf_op jit(solution)/shard_map/norm_grad/pallas_call | solution.py:359
  284.9 1.4 slice_reduce_fusion
  286.3 2.1 copy.15
  (12 shorter events, 0.1 us)
Async XLA Ops:
  7.2 4.4 %copy-start = (bf16[512,768]{1,0:T(8,128)(2,1)S(1)}, bf16[512,768]{1,0:T(8,128)(2,1)}, u32[]{:S(2)}) copy-start(bf16[512,768]{1,0:T(8,128)(2,1)} %h_ref.1) | copy-start | bytes 2359300
  7.2 4.4 %copy-start.3 = (f32[768]{0:T(1024)S(1)}, f32[768]{0:T(1024)}, u32[]{:S(2)}) copy-start(f32[768]{0:T(1024)} %param.9) | copy-start | bytes 9220
  7.2 4.4 %copy-start.2 = (f32[768]{0:T(1024)S(1)}, f32[768]{0:T(1024)}, u32[]{:S(2)}) copy-start(f32[768]{0:T(1024)} %param.8) | copy-start | bytes 9220
  7.2 48.8 %all-gather.3.cloned.1.call-start = ((), (), s32[]{:S(2)}) async-start(), calls=%async_computation.2 | async-start | bytes 7299072 | tf_op jit(solution)/shard_map/all_gather | solution.py:383
  13.0 260.7 %reduce-scatter.2.cloned.1.call-start = ((), (), s32[]{:S(2)}) async-start(), calls=%async_computation.1 | async-start | bytes 14155776 | tf_op jit(solution)/shard_map/reduce_scatter | solution.py:398
  13.1 13.8 %copy-start.1 = (s32[6400]{0:T(1024)S(1)}, s32[6400]{0:T(1024)}, u32[]{:S(2)}) copy-start(s32[6400]{0:T(1024)} %param.11) | copy-start | bytes 76804
Sparse Core Ops, SparseCore 0:
  13.1 42.8 all-gather.2
  205.1 68.5 reduce-scatter.1
